TPU v7x, 256 devices: a whole 4x4x8 slice. The times are simulated.
256 devices in a mesh: gx: 16 (over y, x), gy: 8 (over z_lo, core), ma: 2 (over z_hi).
Axes of the slice: x: 4, y: 4, z: 8 (z_hi: 2, z_lo: 4; z = z_hi * 4 + z_lo), core: 2. Of those that a mesh axis runs over, the one named last changes fastest.
Arguments:
- alpha_fields: bfloat16 [80, 2, 1024, 2048], P('ma', None, 'gy', 'gx'), may hold values from -6 to 6
- member_perts: bfloat16 [80, 2, 1024, 2048], P('ma', None, 'gy', 'gx'), may hold values from -0.625 to 0.625
- band_widths: int32 [2], replicated, may hold values from 2 to 8
- lat_index: int32 [2048], P('gy'), may hold values from 0 to 1022, as said below
- lat_weight: float32 [2048], P('gy'), may hold values from 0 to 1
- lon_index: int32 [4096], P('gx'), may hold values from 0 to 2047, as said below
- lon_weight: float32 [4096], P('gx'), may hold values from 0 to 1
- innovation: float32 [2, 2048, 4096], P(None, 'gy', 'gx'), may hold values from -6 to 6
- obs_weight: float32 [2, 2048, 4096], P(None, 'gy', 'gx'), may hold values from 0.1 to 1
Outputs:
- increment: float32 [2, 2048, 4096], P(None, 'gy', 'gx')
- gradient: float32 [80, 2, 1024, 2048], P('ma', None, 'gy', 'gx')
Inputs may be any that keep to these rules, and one draw needn't show every extreme that they name: lat_index[p] is p // 2 - 1 or p // 2, clamped to 0 .. 1022. lon_index[q] is q // 2 - 1 or q // 2, taken modulo 2048.
All inputs are finite; a program needn't handle non-finite values.
Results may differ from a plain program's by a relative error of at most 0.0003.
Values may be sent and summed in bfloat16 or wider, within the bound.
A program may use at most 128 MiB of HBM per device.

v0:
```python
import functools

import jax
import jax.numpy as jnp
from jax import lax
from jax.experimental import pallas as pl
from jax.experimental.pallas import tpu as pltpu
from jax.sharding import PartitionSpec as P

HB = 8
TILE = 128
EXT = 144
FINE = 256
GROUP = 8
F32 = jnp.float32
BF16 = jnp.bfloat16
MESH = pl.DeviceIdType.MESH
FLOWS = ((1, 0), (-1, 0), (0, 1), (0, -1), (1, 1), (1, -1), (-1, 1), (-1, -1))


def iota(shape, dim):
    return lax.broadcasted_iota(jnp.int32, shape, dim)


def dot(a, b):
    return jnp.dot(a, b, preferred_element_type=F32)


def exact_dot(a, b):
    return jnp.dot(a, b, preferred_element_type=F32, precision=lax.Precision.HIGHEST)


def split(x):
    high = x.astype(BF16)
    return high, (x - high.astype(F32)).astype(BF16)


def taps_at(distance, width):
    spread = jnp.full((8, 128), width.astype(F32), F32)[:1]
    scale = 1.0 / (2.0 * spread * spread)
    offset = (iota((1, 128), 1) - HB).astype(F32)
    shape = jnp.where(iota((1, 128), 1) <= 2 * HB, jnp.exp(-offset * offset * scale), 0.0)
    norm = 1.0 / jnp.sqrt(jnp.sum(shape * shape, axis=1, keepdims=True))
    gap = distance.astype(F32)
    values = jnp.exp(-gap * gap * scale[:, :1]) * norm
    return jnp.where(jnp.abs(distance) <= HB, values, 0.0)


def lon_taps(level, width):
    row = iota((2 * TILE, TILE), 0)
    col = iota((2 * TILE, TILE), 1)
    first = (row & 15) < 8
    west = first if level == 0 else jnp.logical_not(first)
    place = jnp.where(row < TILE, row, jnp.where(west, (row & 7) - HB, TILE + (row & 7)))
    high, low = split(taps_at(place - col, width))
    return jnp.concatenate([high, low], axis=1)


def lat_taps(width):
    row = iota((TILE, 512), 0)
    col = iota((TILE, 512), 1)
    part = (col >= EXT).astype(jnp.int32) + (col >= 2 * EXT).astype(jnp.int32) + (col >= 3 * EXT).astype(jnp.int32)
    k = col - EXT * part
    place = jnp.where(k < TILE, k, jnp.where(k < TILE + HB, k - TILE - HB, k - HB))
    values = taps_at(place - row, width)
    high = values.astype(BF16).astype(F32)
    chosen = jnp.where(part == 2, values - high, jnp.where(part == 3, 0.0, high))
    return chosen.astype(BF16)


def stencil_t(relative, weight):
    cell = iota((FINE, FINE), 0)

    def ext(r):
        return jnp.where(r < 0, r + EXT - HB, jnp.where(r >= TILE, r + HB, r))

    near = jnp.where(cell == ext(relative), 1.0 - weight, 0.0)
    return near + jnp.where(cell == ext(relative + 1), weight, 0.0)


def image_mask(level, j):
    lane = iota((1, TILE), 1)
    start = (lane - 16 * j + (8 if level == 1 else 0)) & 127
    return jnp.where(start < 16, 1.0, 0.0).astype(BF16)


def half_masks():
    lane = iota((1, TILE), 1)
    first = jnp.where((lane & 15) < 8, 1.0, 0.0)
    return first.astype(BF16), (1.0 - first).astype(BF16)


def lat_stack(y):
    high, low = split(y)
    return jnp.concatenate([high, low, high, jnp.zeros((512 - 3 * EXT, TILE), BF16)], axis=0)


def sum_kernel(
    alpha_hbm, perts_hbm, width_ref, lat_i, lat_w, lon_i, lon_w, innov_hbm, weight_hbm,
    inc_out, res_out, edge_out, ph_out, pw_out, pe_out, lon_out, lat_out,
    alpha, perts, ah, ph, pick, apk, ppk, aw, ae, pw, pe, awh, aeh,
    acc, other, coarse, ce, hc, innov, wobs, inc, resm, sel, rows, hm, hs,
    load_sem, a_send, a_recv, p_send, p_recv, m_send, m_recv, c_send, c_recv, r_send, r_recv, out_sem,
):
    gx, gy, ma = lax.axis_index("gx"), lax.axis_index("gy"), lax.axis_index("ma")
    nx, ny = lax.axis_size("gx"), lax.axis_size("gy")
    chunks = alpha.shape[0] // GROUP
    east, west = lax.rem(gx + 1, nx), lax.rem(gx + nx - 1, nx)
    has_up, has_down = gy > 0, gy < ny - 1

    def device(dx, dy):
        return (gx if dx == 0 else (east if dx == 1 else west), gy + dy, ma)

    def guard(dy, body):
        if dy == 0:
            body()
        else:
            pl.when(has_down if dy == 1 else has_up)(body)

    def load(i, b):
        src, dst = ((alpha_hbm, alpha), (perts_hbm, perts))[i]
        rows = pl.ds(b * GROUP, GROUP)
        return pltpu.make_async_copy(src.at[rows], dst.at[rows], load_sem.at[i, b])

    for i in range(2):
        for b in range(chunks):
            load(i, b).start()
    fine_loads = [
        pltpu.make_async_copy(innov_hbm, innov, load_sem.at[2, 0]),
        pltpu.make_async_copy(weight_hbm, wobs, load_sem.at[2, 1]),
    ]
    for copy in fine_loads:
        copy.start()

    barrier = pltpu.get_barrier_semaphore()
    for dx, dy in FLOWS:
        guard(dy, functools.partial(
            pl.semaphore_signal, barrier, inc=1, device_id=device(dx, dy), device_id_type=MESH))
    partner = (gx, gy, 1 - ma)
    pl.semaphore_signal(barrier, inc=1, device_id=partner, device_id_type=MESH)

    row = iota((2 * TILE, 2 * TILE), 0)
    col = iota((2 * TILE, 2 * TILE), 1)
    lane, lev = col & 127, row >> 7
    src = row & 127
    for j in range(GROUP):
        target_e = (16 * j - 8 * lev + src - 120) & 127
        target_w = (16 * j + 8 - 8 * lev + src) & 127
        hit = jnp.where(
            col < TILE,
            jnp.where(src >= 120, (lane == target_e).astype(jnp.int32), 0),
            jnp.where(src < 8, (lane == target_w).astype(jnp.int32), 0),
        )
        pick[j] = hit.astype(F32).astype(BF16)

    def pack(i, fields, packed):
        def one(b, carry):
            load(i, b).wait()
            total = jnp.zeros((TILE, 2 * TILE), F32)
            for j in range(GROUP):
                m = b * GROUP + j
                total = total + dot(jnp.concatenate([fields[m, 0], fields[m, 1]], axis=1), pick[j])
            packed[0, b] = total[:, :TILE].astype(BF16)
            packed[1, b] = total[:, TILE:].astype(BF16)
            return carry

        lax.fori_loop(0, chunks, one, 0)

    def band_copy(f, b, fields, packed, rows_halo, blocks, block_rows, send, recv):
        dx, dy = FLOWS[f]
        edge = pl.ds(TILE - HB, HB) if dy == 1 else pl.ds(0, HB)
        land = pl.ds(0, HB) if dy == 1 else pl.ds(HB, HB)
        members = pl.ds(b * GROUP, GROUP)
        if dx == 0:
            src, dst = fields.at[members, :, edge], rows_halo.at[members, :, land]
        elif dy == 0:
            src, dst = packed.at[0 if dx == 1 else 1, b], blocks[0 if dx == 1 else 1].at[b]
        else:
            src = packed.at[0 if dx == 1 else 1, b, edge]
            dst = block_rows[0 if dx == 1 else 1].at[b, land]
        return pltpu.make_async_remote_copy(
            src_ref=src, dst_ref=dst, send_sem=send.at[f, b], recv_sem=recv.at[f, b],
            device_id=device(dx, dy), device_id_type=MESH)

    a_args = (alpha, apk, ah, (aw, ae), (awh, aeh), a_send, a_recv)
    p_args = (perts, ppk, ph, (pw.at[:, pl.ds(0, TILE)], pe.at[:, pl.ds(0, TILE)]),
              (pw.at[:, pl.ds(TILE, 16)], pe.at[:, pl.ds(TILE, 16)]), p_send, p_recv)

    def each_band(action, args):
        def one(b, carry):
            for f, (dx, dy) in enumerate(FLOWS):
                copy = band_copy(f, b, *args)
                if action == "start":
                    guard(dy, copy.start)
                elif action == "send":
                    guard(dy, copy.wait_send)
                else:
                    guard(-dy, copy.wait_recv)
            return carry

        lax.fori_loop(0, chunks, one, 0)

    pack(0, alpha, apk)
    pl.semaphore_wait(
        barrier, 3 + 3 * has_up.astype(jnp.int32) + 3 * has_down.astype(jnp.int32))
    each_band("start", a_args)

    def clear(first):
        land = pl.ds(0, HB) if first else pl.ds(HB, HB)
        far = pl.ds(TILE, HB) if first else pl.ds(TILE + HB, HB)
        ah[:, :, land] = jnp.zeros((ah.shape[0], 2, HB, TILE), BF16)
        ph[:, :, land] = jnp.zeros((ah.shape[0], 2, HB, TILE), BF16)
        for block in (awh, aeh):
            block[:, land] = jnp.zeros((chunks, HB, TILE), BF16)
        for block in (pw, pe):
            block[:, far] = jnp.zeros((chunks, HB, TILE), BF16)
        dy = 1 if first else -1
        for f, flow in enumerate(FLOWS):
            if flow[1] == dy:
                hc[f] = jnp.zeros((2, HB, TILE), F32)
                hs[f] = jnp.zeros((2, 16, FINE), F32)
        hm[0 if first else 1] = jnp.zeros((2, 16, TILE), F32)

    pl.when(gy == 0)(functools.partial(clear, True))
    pl.when(gy == ny - 1)(functools.partial(clear, False))

    for level in range(2):
        lon_out[level] = lon_taps(level, width_ref[level])
        lat_out[level] = lat_taps(width_ref[level])

    pack(1, perts, ppk)
    each_band("start", p_args)

    mask_a, mask_b = half_masks()

    def partner_copy(level):
        return pltpu.make_async_remote_copy(
            src_ref=acc.at[level], dst_ref=other.at[level], send_sem=m_send.at[level],
            recv_sem=m_recv.at[level], device_id=partner, device_id_type=MESH)

    for level in range(2):
        acc[level] = jnp.zeros((TILE, TILE), F32)

        def chunk(b, carry, level=level):
            if level == 0:
                for f, (dx, dy) in enumerate(FLOWS):
                    guard(-dy, band_copy(f, b, *a_args).wait_recv)
            west_b = jnp.concatenate([aw[b], awh[b]], axis=0)
            east_b = jnp.concatenate([ae[b], aeh[b]], axis=0)
            edges = west_b * mask_a + east_b * mask_b if level == 0 else east_b * mask_a + west_b * mask_b
            total = acc[level]
            for pair in range(GROUP // 2):
                stacks = []
                for j in (2 * pair, 2 * pair + 1):
                    m = b * GROUP + j
                    own = jnp.concatenate([alpha[m, level], ah[m, level]], axis=0)
                    lhs = jnp.concatenate([own, edges * image_mask(level, j)], axis=1)
                    wide = dot(lhs, lon_out[level])
                    stacks.append(lat_stack(wide[:, :TILE] + wide[:, TILE:]))
                z = dot(lat_out[level], jnp.concatenate(stacks, axis=1))
                m = b * GROUP + 2 * pair
                total = total + perts[m, level].astype(F32) * z[:, :TILE]
                total = total + perts[m + 1, level].astype(F32) * z[:, TILE:]
            acc[level] = total
            return carry

        lax.fori_loop(0, chunks, chunk, 0)
        partner_copy(level).start()

    lat_rel = lat_i[...] - gy * TILE
    lon_rel = lax.rem(lon_i[...] - gx * TILE + 1 + nx * TILE, nx * TILE) - 1
    mt = stencil_t(lat_rel, lat_w[...])
    nt = stencil_t(lon_rel, lon_w[...])
    m_map = mt.T
    n_map = nt.T
    zeros_top = jnp.zeros((TILE - HB, FINE), F32)
    top_t = jnp.concatenate([zeros_top, mt[TILE:TILE + HB]], axis=0)
    bottom_t = jnp.concatenate([mt[TILE + HB:EXT], zeros_top], axis=0)
    corner_map = jnp.concatenate([mt[:TILE], top_t, bottom_t], axis=0)

    for level in range(2):
        copy = partner_copy(level)
        copy.wait_recv()
        total = acc[level] + other[level]
        coarse[level] = total
        turned = total.T
        ce[0, level] = turned[TILE - HB:]
        ce[1, level] = turned[:HB]

    def coarse_copy(f):
        dx, dy = FLOWS[f]
        edge = pl.ds(TILE - HB, HB) if dy == 1 else pl.ds(0, HB)
        src = coarse.at[:, edge] if dx == 0 else ce.at[0 if dx == 1 else 1]
        return pltpu.make_async_remote_copy(
            src_ref=src, dst_ref=hc.at[f], send_sem=c_send.at[f], recv_sem=c_recv.at[f],
            device_id=device(dx, dy), device_id_type=MESH)

    for f, (dx, dy) in enumerate(FLOWS):
        guard(dy, coarse_copy(f).start)
    for copy in fine_loads:
        copy.wait()
    for f, (dx, dy) in enumerate(FLOWS):
        guard(-dy, coarse_copy(f).wait_recv)

    for level in range(2):
        framed = jnp.concatenate(
            [coarse[level], hc[2, level], hc[3, level], jnp.zeros((FINE - EXT, TILE), F32)], axis=0)
        by_lat = exact_dot(m_map, framed)
        sides = jnp.concatenate([
            jnp.concatenate([hc[0, level], hc[1, level]], axis=0),
            jnp.concatenate([hc[4, level], hc[6, level]], axis=0),
            jnp.concatenate([hc[5, level], hc[7, level]], axis=0)], axis=1)
        side_t = exact_dot(sides, corner_map)
        side = jnp.concatenate([side_t, jnp.zeros((TILE - 16, FINE), F32)], axis=0).T
        fine = exact_dot(jnp.concatenate([by_lat, side], axis=1), nt)
        inc[level] = fine
        misfit = wobs[level] * (fine - innov[level])
        lon_back = exact_dot(misfit, n_map[:, :TILE])
        chosen = jnp.concatenate([nt[:HB], nt[TILE:TILE + HB], nt[TILE - HB:TILE], nt[TILE + HB:EXT]], axis=0)
        chosen_t = lax.dot_general(
            chosen, misfit, (((1,), (1,)), ((), ())), precision=lax.Precision.HIGHEST,
            preferred_element_type=F32)
        restricted = exact_dot(mt[:EXT], lon_back)
        resm[level] = restricted
        turned = exact_dot(chosen_t, m_map)
        sel[0, level] = turned[16:32]
        sel[1, level] = turned[:16]
        sel[2, level] = jnp.concatenate([turned[8:16], turned[24:32]], axis=0)
        rows[0, level] = jnp.concatenate([restricted[TILE - HB:TILE], restricted[TILE + HB:EXT]], axis=0)
        rows[1, level] = jnp.concatenate([restricted[:HB], restricted[TILE:TILE + HB]], axis=0)

    def edge_copies(f):
        dx, dy = FLOWS[f]
        copies = [pltpu.make_async_remote_copy(
            src_ref=sel.at[2 if dx == 0 else (0 if dx == 1 else 1)], dst_ref=hs.at[f],
            send_sem=r_send.at[f], recv_sem=r_recv.at[f],
            device_id=device(dx, dy), device_id_type=MESH)]
        if dx == 0:
            k = 0 if dy == 1 else 1
            copies.append(pltpu.make_async_remote_copy(
                src_ref=rows.at[k], dst_ref=hm.at[k], send_sem=r_send.at[8 + k], recv_sem=r_recv.at[8 + k],
                device_id=device(dx, dy), device_id_type=MESH))
        return copies

    for f, (dx, dy) in enumerate(FLOWS):
        for copy in edge_copies(f):
            guard(dy, copy.start)
    each_band("recv", p_args)
    results = [
        pltpu.make_async_copy(inc, inc_out, out_sem.at[0]),
        pltpu.make_async_copy(ph, ph_out, out_sem.at[1]),
        pltpu.make_async_copy(pw, pw_out, out_sem.at[2]),
        pltpu.make_async_copy(pe, pe_out, out_sem.at[3]),
    ]
    for copy in results:
        copy.start()
    for f, (dx, dy) in enumerate(FLOWS):
        for copy in edge_copies(f):
            guard(-dy, copy.wait_recv)

    lane = iota((32, FINE), 1)

    def joined(from_west, centre, from_east):
        halo = centre + jnp.concatenate([from_west[:HB], from_east[:HB]], axis=0)
        return jnp.concatenate([halo, from_west[HB:], from_east[HB:]], axis=0)

    def pick_lanes(x, first, first_shift, second, second_shift):
        a = pltpu.roll(x, first_shift, 1)
        b = pltpu.roll(x, second_shift, 1)
        in_a = (lane >= first) & (lane < first + HB)
        in_b = (lane >= second) & (lane < second + HB)
        return jnp.where(in_a, a, jnp.where(in_b, b, 0.0))

    for level in range(2):
        side = joined(hs[0, level], sel[2, level], hs[1, level])
        above = joined(hs[4, level], hs[2, level], hs[6, level])
        below = joined(hs[5, level], hs[3, level], hs[7, level])
        side = side + pick_lanes(above, TILE, 8, 0, 120)
        side = side + pick_lanes(below, TILE + HB, 136, TILE - HB, 248)
        turned = jnp.concatenate([side, jnp.zeros((TILE - 32, FINE), F32)], axis=0).T
        r = iota((TILE, FINE), 0)
        c = iota((TILE, FINE), 1)
        band = (c & 15) if level == 0 else (c & 15) ^ 8
        own = jnp.where(c < HB, c + 16, jnp.where(c >= TILE - HB, c - 96, -1))
        place = jnp.where(r == jnp.where(c < TILE, own, band), 1.0, 0.0)
        spread = exact_dot(turned, place)
        edge_out[level] = spread[:EXT, TILE:]
        top, bottom = hm[0, level], hm[1, level]
        gap = jnp.zeros((TILE - 2 * HB, TILE), F32)
        arrived = jnp.concatenate([top[HB:], gap, bottom[HB:], top[:HB], bottom[:HB]], axis=0)
        res_out[level] = resm[level] + spread[:EXT, :TILE] + arrived

    each_band("send", a_args)
    each_band("send", p_args)
    for level in range(2):
        partner_copy(level).wait_send()
    for f, (dx, dy) in enumerate(FLOWS):
        guard(dy, coarse_copy(f).wait_send)
        for copy in edge_copies(f):
            guard(dy, copy.wait_send)
    for copy in results:
        copy.wait()


def gradient_kernel(alpha, perts, ph, pw, pe, res, edge, lon, lat, inc, grad_out, inc_out):
    mask_a, mask_b = half_masks()
    mask_a, mask_b = mask_a.astype(F32), mask_b.astype(F32)
    inc_out[...] = inc[...]
    for level in range(2):
        west_b, east_b = pw[0].astype(F32), pe[0].astype(F32)
        edges = west_b * mask_a + east_b * mask_b if level == 0 else east_b * mask_a + west_b * mask_b
        edge_high, edge_low = split(edges * edge[level])
        for pair in range(GROUP // 2):
            stacks = []
            for j in (2 * pair, 2 * pair + 1):
                own = jnp.concatenate([perts[j, level], ph[j, level]], axis=0).astype(F32) * res[level]
                high, low = split(own)
                keep = image_mask(level, j)
                wide = dot(jnp.concatenate([high, edge_high * keep], axis=1), lon[level])
                thin = dot(jnp.concatenate([low, edge_low * keep], axis=1), lon[level, :, :TILE])
                stacks.append(lat_stack(wide[:, :TILE] + wide[:, TILE:] + thin))
            z = dot(lat[level], jnp.concatenate(stacks, axis=1))
            j = 2 * pair
            grad_out[j, level] = alpha[j, level].astype(F32) + z[:, :TILE]
            grad_out[j + 1, level] = alpha[j + 1, level].astype(F32) + z[:, TILE:]


def body(alpha, perts, widths, lat_index, lat_weight, lon_index, lon_weight, innovation, obs_weight):
    members = alpha.shape[0]
    chunks = members // GROUP
    any_space = pl.BlockSpec(memory_space=pl.ANY)
    vmem = pl.BlockSpec(memory_space=pltpu.VMEM)
    smem = pl.BlockSpec(memory_space=pltpu.SMEM)
    dma = pltpu.SemaphoreType.DMA
    shapes = [
        jax.ShapeDtypeStruct((2, FINE, FINE), F32),
        jax.ShapeDtypeStruct((2, EXT, TILE), F32),
        jax.ShapeDtypeStruct((2, EXT, TILE), F32),
        jax.ShapeDtypeStruct((members, 2, 16, TILE), BF16),
        jax.ShapeDtypeStruct((chunks, EXT, TILE), BF16),
        jax.ShapeDtypeStruct((chunks, EXT, TILE), BF16),
        jax.ShapeDtypeStruct((2, FINE, FINE), BF16),
        jax.ShapeDtypeStruct((2, TILE, 512), BF16),
    ]
    inc, res, edge, ph, pw, pe, lon, lat = pl.pallas_call(
        sum_kernel,
        out_shape=shapes,
        in_specs=[any_space, any_space, smem, vmem, vmem, vmem, vmem, any_space, any_space],
        out_specs=[any_space, vmem, vmem, any_space, any_space, any_space, vmem, vmem],
        scratch_shapes=[
            pltpu.VMEM(alpha.shape, BF16),
            pltpu.VMEM(alpha.shape, BF16),
            pltpu.VMEM((members, 2, 16, TILE), BF16),
            pltpu.VMEM((members, 2, 16, TILE), BF16),
            pltpu.VMEM((GROUP, FINE, FINE), BF16),
            pltpu.VMEM((2, chunks, TILE, TILE), BF16),
            pltpu.VMEM((2, chunks, TILE, TILE), BF16),
            pltpu.VMEM((chunks, TILE, TILE), BF16),
            pltpu.VMEM((chunks, TILE, TILE), BF16),
            pltpu.VMEM((chunks, EXT, TILE), BF16),
            pltpu.VMEM((chunks, EXT, TILE), BF16),
            pltpu.VMEM((chunks, 16, TILE), BF16),
            pltpu.VMEM((chunks, 16, TILE), BF16),
            pltpu.VMEM((2, TILE, TILE), F32),
            pltpu.VMEM((2, TILE, TILE), F32),
            pltpu.VMEM((2, TILE, TILE), F32),
            pltpu.VMEM((2, 2, HB, TILE), F32),
            pltpu.VMEM((8, 2, HB, TILE), F32),
            pltpu.VMEM((2, FINE, FINE), F32),
            pltpu.VMEM((2, FINE, FINE), F32),
            pltpu.VMEM((2, FINE, FINE), F32),
            pltpu.VMEM((2, EXT, TILE), F32),
            pltpu.VMEM((3, 2, 16, FINE), F32),
            pltpu.VMEM((2, 2, 16, TILE), F32),
            pltpu.VMEM((2, 2, 16, TILE), F32),
            pltpu.VMEM((8, 2, 16, FINE), F32),
            dma((3, chunks)),
            dma((8, chunks)), dma((8, chunks)), dma((8, chunks)), dma((8, chunks)),
            dma((2,)), dma((2,)), dma((8,)), dma((8,)), dma((10,)), dma((10,)), dma((4,)),
        ],
        compiler_params=pltpu.CompilerParams(
            collective_id=0, has_side_effects=True, vmem_limit_bytes=48 * 2**20),
        name="sum_kernel",
    )(
        alpha, perts, widths, lat_index[None], lat_weight[None], lon_index[None], lon_weight[None],
        innovation, obs_weight,
    )
    group = pl.BlockSpec((GROUP, 2, TILE, TILE), lambda b: (b, 0, 0, 0))
    block = pl.BlockSpec((1, EXT, TILE), lambda b: (b, 0, 0))

    def whole(x):
        return pl.BlockSpec(x.shape, lambda b: (0, 0, 0))

    gradient, increment = pl.pallas_call(
        gradient_kernel,
        grid=(chunks,),
        out_shape=[
            jax.ShapeDtypeStruct(alpha.shape, F32),
            jax.ShapeDtypeStruct((2, FINE, FINE), F32),
        ],
        in_specs=[
            group, group, pl.BlockSpec((GROUP, 2, 16, TILE), lambda b: (b, 0, 0, 0)),
            block, block, whole(res), whole(edge), whole(lon), whole(lat), whole(inc),
        ],
        out_specs=[group, whole(inc)],
        compiler_params=pltpu.CompilerParams(
            dimension_semantics=("arbitrary",), vmem_limit_bytes=48 * 2**20),
        name="gradient_kernel",
    )(alpha, perts, ph, pw, pe, res, edge, lon, lat, inc)
    return (increment, gradient)


def solution(mesh):
    placed = (
        P("ma", None, "gy", "gx"),
        P("ma", None, "gy", "gx"),
        P(),
        P("gy"),
        P("gy"),
        P("gx"),
        P("gx"),
        P(None, "gy", "gx"),
        P(None, "gy", "gx"),
    )
    return jax.shard_map(
        body,
        mesh=mesh,
        in_specs=placed,
        out_specs=(P(None, "gy", "gx"), P("ma", None, "gy", "gx")),
        check_vma=False,
    )
```

profile of v0, /device:TPU:1, one launch (start us, length us, event | category | flops | bytes accessed | tf_op | source)
XLA Modules:
  0.0 67.6 jit_solution(1039438902225179312)
XLA Ops:
  0.6 0.0 copy-start
  0.6 1.7 %copy-done = bf16[40,2,128,128]{3,2,1,0:T(8,128)(2,1)S(1)} copy-done((bf16[40,2,128,128]{3,2,1,0:T(8,128)(2,1)S(1)}, bf16[40,2,128,128]{3,2,1,0:T(8,128)(2,1)}, u32[]{:S(2)}) %copy-start) | copy-done | bytes 2621464
  2.4 0.0 copy-start.1
  2.4 1.0 %copy-done.1 = f32[2,256,256]{2,1,0:T(8,128)S(1)} copy-done((f32[2,256,256]{2,1,0:T(8,128)S(1)}, f32[2,256,256]{2,1,0:T(8,128)}, u32[]{:S(2)}) %copy-start.1) | copy-done | bytes 524312
  3.4 0.0 copy-start.2
  3.4 1.0 %copy-done.2 = f32[2,256,256]{2,1,0:T(8,128)S(1)} copy-done((f32[2,256,256]{2,1,0:T(8,128)S(1)}, f32[2,256,256]{2,1,0:T(8,128)}, u32[]{:S(2)}) %copy-start.2) | copy-done | bytes 524312
  4.5 0.0 copy-start.3
  4.5 0.7 %copy-done.3 = s32[256]{0:T(256)S(1)} copy-done((s32[256]{0:T(256)S(1)}, s32[256]{0:T(256)}, u32[]{:S(2)}) %copy-start.3) | copy-done | bytes 1048
  5.1 0.0 copy-start.4
  5.1 0.7 %copy-done.4 = f32[256]{0:T(256)S(1)} copy-done((f32[256]{0:T(256)S(1)}, f32[256]{0:T(256)}, u32[]{:S(2)}) %copy-start.4) | copy-done | bytes 1048
  5.8 0.0 copy-start.5
  5.8 0.7 %copy-done.5 = s32[256]{0:T(256)S(1)} copy-done((s32[256]{0:T(256)S(1)}, s32[256]{0:T(256)}, u32[]{:S(2)}) %copy-start.5) | copy-done | bytes 1048
  6.5 0.0 copy-start.6
  6.5 0.7 %copy-done.6 = f32[256]{0:T(256)S(1)} copy-done((f32[256]{0:T(256)S(1)}, f32[256]{0:T(256)}, u32[]{:S(2)}) %copy-start.6) | copy-done | bytes 1048
  7.2 0.0 copy-start.7
  7.2 0.7 copy-done.7
  7.8 45.2 %sum_kernel.1 = (f32[2,256,256]{2,1,0:T(8,128)S(1)}, f32[2,144,128]{2,1,0:T(8,128)S(1)}, f32[2,144,128]{2,1,0:T(8,128)S(1)}, bf16[40,2,16,128]{3,2,1,0:T(8,128)(...) custom-call(bf16[40,2,128,128]{3,2,1,0:T(8,128)(2,1)S(1)} %copy-done, ...), custom_call_target="tpu_custom_call" | custom-call | tf_op jit(solution)/shard_map/sum_kernel/pallas_call | solution.py:445
  53.1 14.6 %gradient_kernel.1 = (f32[40,2,128,128]{3,2,1,0:T(8,128)}, f32[2,256,256]{2,1,0:T(8,128)}) custom-call(bf16[40,2,128,128]{3,2,1,0:T(8,128)(2,1)S(1)} %copy-done, bf16[40,2,128,128]{3,2,1,0:T(8,128)(2,1)} %perts.1, bf16[40,2,16,128]{3,2,1,0:T(8,128)(2,1)S(1)} %get-tuple-element.12.ph, bf16[5,144,128]{2,1,0:T(8,128)(2,1)S(1)} %get-tuple-element.13.pw, ...), custom_call_target="tpu_custom_call" | custom-call | tf_op jit(solution)/shard_map/gradient_kernel/pallas_call | solution.py:494
Async XLA Ops:
  0.6 1.7 %copy-start = (bf16[40,2,128,128]{3,2,1,0:T(8,128)(2,1)S(1)}, bf16[40,2,128,128]{3,2,1,0:T(8,128)(2,1)}, u32[]{:S(2)}) copy-start(bf16[40,2,128,128]{3,2,1,0:T(8,128)(2,1)} %alpha.1) | copy-start | bytes 7864324
  2.4 1.0 %copy-start.1 = (f32[2,256,256]{2,1,0:T(8,128)S(1)}, f32[2,256,256]{2,1,0:T(8,128)}, u32[]{:S(2)}) copy-start(f32[2,256,256]{2,1,0:T(8,128)} %innov_hbm.1) | copy-start | bytes 1572868
  3.4 1.0 %copy-start.2 = (f32[2,256,256]{2,1,0:T(8,128)S(1)}, f32[2,256,256]{2,1,0:T(8,128)}, u32[]{:S(2)}) copy-start(f32[2,256,256]{2,1,0:T(8,128)} %weight_hbm.1) | copy-start | bytes 1572868
  4.5 0.7 %copy-start.3 = (s32[256]{0:T(256)S(1)}, s32[256]{0:T(256)}, u32[]{:S(2)}) copy-start(s32[256]{0:T(256)} %param.12) | copy-start | bytes 3076
  5.1 0.7 %copy-start.4 = (f32[256]{0:T(256)S(1)}, f32[256]{0:T(256)}, u32[]{:S(2)}) copy-start(f32[256]{0:T(256)} %param.13) | copy-start | bytes 3076
  5.8 0.7 %copy-start.5 = (s32[256]{0:T(256)S(1)}, s32[256]{0:T(256)}, u32[]{:S(2)}) copy-start(s32[256]{0:T(256)} %param.14) | copy-start | bytes 3076
  6.5 0.7 %copy-start.6 = (f32[256]{0:T(256)S(1)}, f32[256]{0:T(256)}, u32[]{:S(2)}) copy-start(f32[256]{0:T(256)} %param.15) | copy-start | bytes 3076
  7.2 0.7 copy-start.7
where the time goes:
time: 67.9 us; the launch traced here: 67.6 us
  Pallas kernels  59.8 us (88%)
  local copies, waits for them, and re-layouts  7.18 us (11%)
    pallas_call x1, Pallas kernels, body(): pl.pallas_call(sum_kernel, out_shape=shapes, in_specs=[any_space, any_spa...  45.2 us
    pallas_call x1, Pallas kernels, body(): pl.pallas_call(gradient_kernel, grid=(chunks,), out_shape=[jax.ShapeDtype...  14.6 us
    unnamed x16, local copies, waits for them, and re-layouts  7.18 us

commit v1 on v0

v1 whole, which is shorter than its diff:
```python
import functools

import jax
import jax.numpy as jnp
from jax import lax
from jax.experimental import pallas as pl
from jax.experimental.pallas import tpu as pltpu
from jax.sharding import PartitionSpec as P

HB = 8
TILE = 128
EXT = 144
FINE = 256
GROUP = 8
F32 = jnp.float32
BF16 = jnp.bfloat16
MESH = pl.DeviceIdType.MESH
FLOWS = ((1, 0), (-1, 0), (0, 1), (0, -1), (1, 1), (1, -1), (-1, 1), (-1, -1))


def iota(shape, dim):
    return lax.broadcasted_iota(jnp.int32, shape, dim)


def dot(a, b):
    return jnp.dot(a, b, preferred_element_type=F32)


def split(x):
    high = x.astype(BF16)
    return high, (x - high.astype(F32)).astype(BF16)


def dot3(a, b):
    return dot(a[0], b[0]) + dot(a[0], b[1]) + dot(a[1], b[0])


def taps_at(distance, width):
    spread = jnp.full((8, 128), width.astype(F32), F32)[:1]
    scale = 1.0 / (2.0 * spread * spread)
    offset = (iota((1, 128), 1) - HB).astype(F32)
    shape = jnp.where(iota((1, 128), 1) <= 2 * HB, jnp.exp(-offset * offset * scale), 0.0)
    norm = 1.0 / jnp.sqrt(jnp.sum(shape * shape, axis=1, keepdims=True))
    gap = distance.astype(F32)
    values = jnp.exp(-gap * gap * scale[:, :1]) * norm
    return jnp.where(jnp.abs(distance) <= HB, values, 0.0)


def lon_taps(level, width):
    row = iota((2 * TILE, TILE), 0)
    col = iota((2 * TILE, TILE), 1)
    first = (row & 15) < 8
    west = first if level == 0 else jnp.logical_not(first)
    place = jnp.where(row < TILE, row, jnp.where(west, (row & 7) - HB, TILE + (row & 7)))
    high, low = split(taps_at(place - col, width))
    return jnp.concatenate([
        jnp.concatenate([high, low], axis=1), jnp.concatenate([high, jnp.zeros_like(high)], axis=1)], axis=0)


def lat_taps(width):
    row = iota((TILE, 512), 0)
    col = iota((TILE, 512), 1)
    part = (col >= EXT).astype(jnp.int32) + (col >= 2 * EXT).astype(jnp.int32) + (col >= 3 * EXT).astype(jnp.int32)
    k = col - EXT * part
    place = jnp.where(k < TILE, k, jnp.where(k < TILE + HB, k - TILE - HB, k - HB))
    values = taps_at(place - row, width)
    high = values.astype(BF16).astype(F32)
    chosen = jnp.where(part == 2, values - high, jnp.where(part == 3, 0.0, high))
    return chosen.astype(BF16)


def stencil_t(relative, weight):
    cell = iota((FINE, FINE), 0)

    def ext(r):
        return jnp.where(r < 0, r + EXT - HB, jnp.where(r >= TILE, r + HB, r))

    near = jnp.where(cell == ext(relative), 1.0 - weight, 0.0)
    return near + jnp.where(cell == ext(relative + 1), weight, 0.0)


def image_mask(level, j):
    lane = iota((1, TILE), 1)
    start = (lane - 16 * j + (8 if level == 1 else 0)) & 127
    return jnp.where(start < 16, 1.0, 0.0).astype(BF16)


def half_masks():
    lane = iota((1, TILE), 1)
    first = jnp.where((lane & 15) < 8, 1.0, 0.0)
    return first.astype(BF16), (1.0 - first).astype(BF16)


def keep_stack(stack, i, y):
    high, low = split(y)
    for k, part in enumerate((high, low, high)):
        stack[k * EXT:(k + 1) * EXT, i * TILE:(i + 1) * TILE] = part


def sum_kernel(
    alpha_hbm, perts_hbm, width_hbm, lat_i_hbm, lat_w_hbm, lon_i_hbm, lon_w_hbm, innov_hbm, weight_hbm,
    inc, res_out, edge_out, ph_out, pw_out, pe_out, lon_out, lat_out, alpha, perts,
    ah, ph, pick, apk, ppk, aw, ae, pw, pe, awh, aeh, stack,
    acc, other, coarse, ce, hc, innov, wobs, resm, sel, rows, hm, hs,
    width_ref, lat_i, lat_w, lon_i, lon_w, mt2, m2, nt2, n2, corner2, place,
    load_sem, a_send, a_recv, p_send, p_recv, m_send, m_recv, c_send, c_recv, r_send, r_recv,
):
    gx, gy, ma = lax.axis_index("gx"), lax.axis_index("gy"), lax.axis_index("ma")
    nx, ny = lax.axis_size("gx"), lax.axis_size("gy")
    chunks = alpha.shape[0] // GROUP
    east, west = lax.rem(gx + 1, nx), lax.rem(gx + nx - 1, nx)
    has_up, has_down = gy > 0, gy < ny - 1

    def device(dx, dy):
        return (gx if dx == 0 else (east if dx == 1 else west), gy + dy, ma)

    def guard(dy, body):
        if dy == 0:
            body()
        else:
            pl.when(has_down if dy == 1 else has_up)(body)

    def load(i, b):
        src, dst = ((alpha_hbm, alpha), (perts_hbm, perts))[i]
        rows = pl.ds(b * GROUP, GROUP)
        return pltpu.make_async_copy(src.at[rows], dst.at[rows], load_sem.at[i, b])

    for i in range(2):
        for b in range(chunks):
            load(i, b).start()
    small_loads = [
        pltpu.make_async_copy(src, dst, load_sem.at[3, k])
        for k, (src, dst) in enumerate((
            (lat_i_hbm, lat_i), (lat_w_hbm, lat_w), (lon_i_hbm, lon_i), (lon_w_hbm, lon_w)))
    ]
    width_load = pltpu.make_async_copy(width_hbm, width_ref, load_sem.at[2, 2])
    for copy in (*small_loads, width_load):
        copy.start()
    fine_loads = [
        pltpu.make_async_copy(innov_hbm, innov, load_sem.at[2, 0]),
        pltpu.make_async_copy(weight_hbm, wobs, load_sem.at[2, 1]),
    ]
    for copy in fine_loads:
        copy.start()

    barrier = pltpu.get_barrier_semaphore()
    for dx, dy in FLOWS:
        guard(dy, functools.partial(
            pl.semaphore_signal, barrier, inc=1, device_id=device(dx, dy), device_id_type=MESH))
    partner = (gx, gy, 1 - ma)
    pl.semaphore_signal(barrier, inc=1, device_id=partner, device_id_type=MESH)

    row = iota((2 * TILE, 2 * TILE), 0)
    col = iota((2 * TILE, 2 * TILE), 1)
    lane, lev = col & 127, row >> 7
    src = row & 127
    for j in range(GROUP):
        target_e = (16 * j - 8 * lev + src - 120) & 127
        target_w = (16 * j + 8 - 8 * lev + src) & 127
        hit = jnp.where(
            col < TILE,
            jnp.where(src >= 120, (lane == target_e).astype(jnp.int32), 0),
            jnp.where(src < 8, (lane == target_w).astype(jnp.int32), 0),
        )
        pick[j] = hit.astype(F32).astype(BF16)

    def pack(i, fields, packed):
        def one(b, carry):
            load(i, b).wait()
            total = jnp.zeros((TILE, 2 * TILE), F32)
            for j in range(GROUP):
                m = b * GROUP + j
                total = total + dot(jnp.concatenate([fields[m, 0], fields[m, 1]], axis=1), pick[j])
            packed[0, b] = total[:, :TILE].astype(BF16)
            packed[1, b] = total[:, TILE:].astype(BF16)
            return carry

        lax.fori_loop(0, chunks, one, 0)

    def band_copy(f, b, fields, packed, rows_halo, blocks, block_rows, send, recv):
        dx, dy = FLOWS[f]
        edge = pl.ds(TILE - HB, HB) if dy == 1 else pl.ds(0, HB)
        land = pl.ds(0, HB) if dy == 1 else pl.ds(HB, HB)
        members = pl.ds(b * GROUP, GROUP)
        if dx == 0:
            src, dst = fields.at[members, :, edge], rows_halo.at[members, :, land]
        elif dy == 0:
            src, dst = packed.at[0 if dx == 1 else 1, b], blocks[0 if dx == 1 else 1].at[b]
        else:
            src = packed.at[0 if dx == 1 else 1, b, edge]
            dst = block_rows[0 if dx == 1 else 1].at[b, land]
        return pltpu.make_async_remote_copy(
            src_ref=src, dst_ref=dst, send_sem=send.at[f, b], recv_sem=recv.at[f, b],
            device_id=device(dx, dy), device_id_type=MESH)

    a_args = (alpha, apk, ah, (aw, ae), (awh, aeh), a_send, a_recv)
    p_args = (perts, ppk, ph, (pw.at[:, pl.ds(0, TILE)], pe.at[:, pl.ds(0, TILE)]),
              (pw.at[:, pl.ds(TILE, 16)], pe.at[:, pl.ds(TILE, 16)]), p_send, p_recv)

    def each_band(action, args):
        def one(b, carry):
            for f, (dx, dy) in enumerate(FLOWS):
                copy = band_copy(f, b, *args)
                if action == "start":
                    guard(dy, copy.start)
                elif action == "send":
                    guard(dy, copy.wait_send)
                else:
                    guard(-dy, copy.wait_recv)
            return carry

        lax.fori_loop(0, chunks, one, 0)

    pack(0, alpha, apk)
    pl.semaphore_wait(
        barrier, 3 + 3 * has_up.astype(jnp.int32) + 3 * has_down.astype(jnp.int32))
    each_band("start", a_args)

    def clear(first):
        land = pl.ds(0, HB) if first else pl.ds(HB, HB)
        far = pl.ds(TILE, HB) if first else pl.ds(TILE + HB, HB)
        ah[:, :, land] = jnp.zeros((ah.shape[0], 2, HB, TILE), BF16)
        ph[:, :, land] = jnp.zeros((ah.shape[0], 2, HB, TILE), BF16)
        for block in (awh, aeh):
            block[:, land] = jnp.zeros((chunks, HB, TILE), BF16)
        for block in (pw, pe):
            block[:, far] = jnp.zeros((chunks, HB, TILE), BF16)
        dy = 1 if first else -1
        for f, flow in enumerate(FLOWS):
            if flow[1] == dy:
                hc[f] = jnp.zeros((2, HB, TILE), F32)
                hs[f] = jnp.zeros((2, 16, FINE), F32)
        hm[0 if first else 1] = jnp.zeros((2, 16, TILE), F32)

    pl.when(gy == 0)(functools.partial(clear, True))
    pl.when(gy == ny - 1)(functools.partial(clear, False))

    stack[:, 3 * EXT:] = jnp.zeros((2, 512 - 3 * EXT, GROUP * TILE), BF16)
    width_load.wait()
    for level in range(2):
        lon_out[level] = lon_taps(level, width_ref[level])
        lat_out[level] = lat_taps(width_ref[level])

    pack(1, perts, ppk)
    each_band("start", p_args)

    for copy in small_loads:
        copy.wait()
    lat_rel = lat_i[...] - gy * TILE
    lon_rel = lax.rem(lon_i[...] - gx * TILE + 1 + nx * TILE, nx * TILE) - 1
    mt = stencil_t(lat_rel, lat_w[...])
    nt = stencil_t(lon_rel, lon_w[...])
    zeros_top = jnp.zeros((TILE - HB, FINE), F32)
    top_t = jnp.concatenate([zeros_top, mt[TILE:TILE + HB]], axis=0)
    bottom_t = jnp.concatenate([mt[TILE + HB:EXT], zeros_top], axis=0)
    corner = jnp.concatenate([mt[:TILE], top_t, bottom_t], axis=0)
    for table, value in ((mt2, mt), (m2, mt.T), (nt2, nt), (n2, nt.T), (corner2, corner)):
        table[0], table[1] = split(value)
    r = iota((TILE, FINE), 0)
    c = iota((TILE, FINE), 1)
    for level in range(2):
        band = (c & 15) if level == 0 else (c & 15) ^ 8
        own = jnp.where(c < HB, c + 16, jnp.where(c >= TILE - HB, c - 96, -1))
        place[level] = jnp.where(r == jnp.where(c < TILE, own, band), 1.0, 0.0).astype(BF16)

    mask_a, mask_b = half_masks()

    def partner_copy(level):
        return pltpu.make_async_remote_copy(
            src_ref=acc.at[level], dst_ref=other.at[level], send_sem=m_send.at[level],
            recv_sem=m_recv.at[level], device_id=partner, device_id_type=MESH)

    def add_chunk(b, level):
        west_b = jnp.concatenate([aw[b], awh[b]], axis=0)
        east_b = jnp.concatenate([ae[b], aeh[b]], axis=0)
        edges = west_b * mask_a + east_b * mask_b if level == 0 else east_b * mask_a + west_b * mask_b
        for j in range(GROUP):
            m = b * GROUP + j
            own = jnp.concatenate([alpha[m, level], ah[m, level]], axis=0)
            lhs = jnp.concatenate([own, edges * image_mask(level, j)], axis=1)
            wide = dot(lhs, lon_out[level, :2 * TILE])
            keep_stack(stack.at[level], j, wide[:, :TILE] + wide[:, TILE:])
        total = acc[level]
        for pair in range(GROUP // 2):
            z = dot(lat_out[level], stack[level, :, pair * FINE:(pair + 1) * FINE])
            m = b * GROUP + 2 * pair
            total = total + perts[m, level].astype(F32) * z[:, :TILE]
            total = total + perts[m + 1, level].astype(F32) * z[:, TILE:]
        acc[level] = total

    def arrive(b):
        for f, (dx, dy) in enumerate(FLOWS):
            guard(-dy, band_copy(f, b, *a_args).wait_recv)

    def chunk(b, carry):
        arrive(b)
        for level in range(2):
            add_chunk(b, level)
        return carry

    acc[...] = jnp.zeros((2, TILE, TILE), F32)
    lax.fori_loop(0, chunks - 1, chunk, 0)
    arrive(chunks - 1)
    for level in range(2):
        add_chunk(chunks - 1, level)
        partner_copy(level).start()

    def coarse_copy(f, level):
        dx, dy = FLOWS[f]
        edge = pl.ds(TILE - HB, HB) if dy == 1 else pl.ds(0, HB)
        src = coarse.at[level, edge] if dx == 0 else ce.at[0 if dx == 1 else 1, level]
        return pltpu.make_async_remote_copy(
            src_ref=src, dst_ref=hc.at[f, level], send_sem=c_send.at[f, level],
            recv_sem=c_recv.at[f, level], device_id=device(dx, dy), device_id_type=MESH)

    def edge_copies(f, level):
        dx, dy = FLOWS[f]
        copies = [pltpu.make_async_remote_copy(
            src_ref=sel.at[2 if dx == 0 else (0 if dx == 1 else 1), level], dst_ref=hs.at[f, level],
            send_sem=r_send.at[f, level], recv_sem=r_recv.at[f, level],
            device_id=device(dx, dy), device_id_type=MESH)]
        if dx == 0:
            k = 0 if dy == 1 else 1
            copies.append(pltpu.make_async_remote_copy(
                src_ref=rows.at[k, level], dst_ref=hm.at[k, level], send_sem=r_send.at[8 + k, level],
                recv_sem=r_recv.at[8 + k, level], device_id=device(dx, dy), device_id_type=MESH))
        return copies

    def total_step(level):
        partner_copy(level).wait_recv()
        total = acc[level] + other[level]
        coarse[level] = total
        turned = total.T
        ce[0, level] = turned[TILE - HB:]
        ce[1, level] = turned[:HB]
        for f, (dx, dy) in enumerate(FLOWS):
            guard(dy, coarse_copy(f, level).start)

    def fine_step(level):
        for f, (dx, dy) in enumerate(FLOWS):
            guard(-dy, coarse_copy(f, level).wait_recv)
        framed = jnp.concatenate(
            [coarse[level], hc[2, level], hc[3, level], jnp.zeros((FINE - EXT, TILE), F32)], axis=0)
        by_lat = dot3(m2, split(framed))
        sides = jnp.concatenate([
            jnp.concatenate([hc[0, level], hc[1, level]], axis=0),
            jnp.concatenate([hc[4, level], hc[6, level]], axis=0),
            jnp.concatenate([hc[5, level], hc[7, level]], axis=0)], axis=1)
        side_t = dot3(split(sides), corner2)
        side = jnp.concatenate([side_t, jnp.zeros((TILE - 16, FINE), F32)], axis=0).T
        fine = dot3(split(jnp.concatenate([by_lat, side], axis=1)), nt2)
        inc[level] = fine
        misfit = split(wobs[level] * (fine - innov[level]))
        lon_back = split(dot3(misfit, (n2[0, :, :TILE], n2[1, :, :TILE])))

        def turned_dot(part, values):
            table = jnp.concatenate([
                part[:HB], part[TILE:TILE + HB], part[TILE - HB:TILE], part[TILE + HB:EXT]], axis=0)
            return lax.dot_general(
                table.astype(BF16), values, (((1,), (1,)), ((), ())), preferred_element_type=F32)

        high, low = nt2[0].astype(F32), nt2[1].astype(F32)
        chosen_t = turned_dot(high, misfit[0]) + turned_dot(high, misfit[1]) + turned_dot(low, misfit[0])
        restricted = dot3((mt2[0, :EXT], mt2[1, :EXT]), lon_back)
        resm[level] = restricted
        turned = dot3(split(chosen_t), m2)
        sel[0, level] = turned[16:32]
        sel[1, level] = turned[:16]
        sel[2, level] = jnp.concatenate([turned[8:16], turned[24:32]], axis=0)
        rows[0, level] = jnp.concatenate([restricted[TILE - HB:TILE], restricted[TILE + HB:EXT]], axis=0)
        rows[1, level] = jnp.concatenate([restricted[:HB], restricted[TILE:TILE + HB]], axis=0)
        for f, (dx, dy) in enumerate(FLOWS):
            for copy in edge_copies(f, level):
                guard(dy, copy.start)

    lane = iota((32, FINE), 1)

    def joined(from_west, centre, from_east):
        halo = centre + jnp.concatenate([from_west[:HB], from_east[:HB]], axis=0)
        return jnp.concatenate([halo, from_west[HB:], from_east[HB:]], axis=0)

    def pick_lanes(x, first, first_shift, second, second_shift):
        a = pltpu.roll(x, first_shift, 1)
        b = pltpu.roll(x, second_shift, 1)
        in_a = (lane >= first) & (lane < first + HB)
        in_b = (lane >= second) & (lane < second + HB)
        return jnp.where(in_a, a, jnp.where(in_b, b, 0.0))

    def residual_step(level):
        for f, (dx, dy) in enumerate(FLOWS):
            for copy in edge_copies(f, level):
                guard(-dy, copy.wait_recv)
        side = joined(hs[0, level], sel[2, level], hs[1, level])
        above = joined(hs[4, level], hs[2, level], hs[6, level])
        below = joined(hs[5, level], hs[3, level], hs[7, level])
        side = side + pick_lanes(above, TILE, 8, 0, 120)
        side = side + pick_lanes(below, TILE + HB, 136, TILE - HB, 248)
        turned = split(jnp.concatenate([side, jnp.zeros((TILE - 32, FINE), F32)], axis=0).T)
        spread = dot(turned[0], place[level]) + dot(turned[1], place[level])
        edge_out[level] = spread[:EXT, TILE:]
        top, bottom = hm[0, level], hm[1, level]
        gap = jnp.zeros((TILE - 2 * HB, TILE), F32)
        arrived = jnp.concatenate([top[HB:], gap, bottom[HB:], top[:HB], bottom[:HB]], axis=0)
        res_out[level] = resm[level] + spread[:EXT, :TILE] + arrived

    total_step(0)
    total_step(1)
    for copy in fine_loads:
        copy.wait()
    fine_step(0)
    fine_step(1)
    each_band("recv", p_args)
    ph_out[...] = ph[...]
    pw_out[...] = pw[...]
    pe_out[...] = pe[...]
    residual_step(0)
    residual_step(1)
    each_band("send", a_args)
    each_band("send", p_args)
    for level in range(2):
        partner_copy(level).wait_send()
        for f, (dx, dy) in enumerate(FLOWS):
            guard(dy, coarse_copy(f, level).wait_send)
            for copy in edge_copies(f, level):
                guard(dy, copy.wait_send)


def gradient_kernel(
    alpha, perts, ph, pw, pe, res, edge, lon, lat, inc, grad_out, inc_out, lhs, stack, result, grad_sem, inc_sem,
):
    inc_copy = pltpu.make_async_copy(inc, inc_out, inc_sem)
    inc_copy.start()
    mask_a, mask_b = (mask.astype(F32) for mask in half_masks())
    stack[:, 3 * EXT:] = jnp.zeros((2, 512 - 3 * EXT, GROUP * TILE), BF16)

    def out_copy(b, level):
        members = pl.ds(b * GROUP, GROUP)
        return pltpu.make_async_copy(
            result.at[members, level], grad_out.at[members, level], grad_sem.at[level, b])

    def chunk(b, carry):
        west_b, east_b = pw[b].astype(F32), pe[b].astype(F32)
        for level in range(2):
            edges = west_b * mask_a + east_b * mask_b if level == 0 else east_b * mask_a + west_b * mask_b
            edge_high, edge_low = split(edges * edge[level])
            for j in range(GROUP):
                m = b * GROUP + j
                own = jnp.concatenate([perts[m, level], ph[m, level]], axis=0).astype(F32) * res[level]
                high, low = split(own)
                keep = image_mask(level, j)
                for k, part in enumerate((high, edge_high * keep, low, edge_low * keep)):
                    lhs[level, j * EXT:(j + 1) * EXT, k * TILE:(k + 1) * TILE] = part
            for j in range(GROUP):
                wide = dot(lhs[level, j * EXT:(j + 1) * EXT], lon[level])
                keep_stack(stack.at[level], j, wide[:, :TILE] + wide[:, TILE:])
            for pair in range(GROUP // 2):
                z = dot(lat[level], stack[level, :, pair * FINE:(pair + 1) * FINE])
                m = b * GROUP + 2 * pair
                result[m, level] = alpha[m, level].astype(F32) + z[:, :TILE]
                result[m + 1, level] = alpha[m + 1, level].astype(F32) + z[:, TILE:]
            out_copy(b, level).start()
        return carry

    chunks = pw.shape[0]
    lax.fori_loop(0, chunks, chunk, 0)
    for b in range(chunks):
        for level in range(2):
            out_copy(b, level).wait()
    inc_copy.wait()


def body(alpha, perts, widths, lat_index, lat_weight, lon_index, lon_weight, innovation, obs_weight):
    members = alpha.shape[0]
    chunks = members // GROUP
    hbm = pl.BlockSpec(memory_space=pltpu.HBM)
    vmem = pl.BlockSpec(memory_space=pltpu.VMEM)
    dma = pltpu.SemaphoreType.DMA
    fine = (2, FINE, FINE)
    shapes = [
        pltpu.VMEM(fine, F32),
        pltpu.VMEM((2, EXT, TILE), F32),
        pltpu.VMEM((2, EXT, TILE), F32),
        pltpu.VMEM((members, 2, 16, TILE), BF16),
        pltpu.VMEM((chunks, EXT, TILE), BF16),
        pltpu.VMEM((chunks, EXT, TILE), BF16),
        pltpu.VMEM((2, 2 * FINE, FINE), BF16),
        pltpu.VMEM((2, TILE, 2 * FINE), BF16),
        pltpu.VMEM(alpha.shape, BF16),
        pltpu.VMEM(alpha.shape, BF16),
    ]
    inc, res, edge, ph, pw, pe, lon, lat, alpha_v, perts_v = pl.pallas_call(
        sum_kernel,
        out_shape=shapes,
        in_specs=[hbm] * 9,
        out_specs=[vmem] * len(shapes),
        scratch_shapes=[
            pltpu.VMEM((members, 2, 16, TILE), BF16),
            pltpu.VMEM((members, 2, 16, TILE), BF16),
            pltpu.VMEM((GROUP, FINE, FINE), BF16),
            pltpu.VMEM((2, chunks, TILE, TILE), BF16),
            pltpu.VMEM((2, chunks, TILE, TILE), BF16),
            pltpu.VMEM((chunks, TILE, TILE), BF16),
            pltpu.VMEM((chunks, TILE, TILE), BF16),
            pltpu.VMEM((chunks, EXT, TILE), BF16),
            pltpu.VMEM((chunks, EXT, TILE), BF16),
            pltpu.VMEM((chunks, 16, TILE), BF16),
            pltpu.VMEM((chunks, 16, TILE), BF16),
            pltpu.VMEM((2, 2 * FINE, GROUP * TILE), BF16),
            pltpu.VMEM((2, TILE, TILE), F32),
            pltpu.VMEM((2, TILE, TILE), F32),
            pltpu.VMEM((2, TILE, TILE), F32),
            pltpu.VMEM((2, 2, HB, TILE), F32),
            pltpu.VMEM((8, 2, HB, TILE), F32),
            pltpu.VMEM(fine, F32),
            pltpu.VMEM(fine, F32),
            pltpu.VMEM((2, EXT, TILE), F32),
            pltpu.VMEM((3, 2, 16, FINE), F32),
            pltpu.VMEM((2, 2, 16, TILE), F32),
            pltpu.VMEM((2, 2, 16, TILE), F32),
            pltpu.VMEM((8, 2, 16, FINE), F32),
            pltpu.SMEM((2,), jnp.int32),
            pltpu.VMEM((1, FINE), jnp.int32),
            pltpu.VMEM((1, FINE), F32),
            pltpu.VMEM((1, FINE), jnp.int32),
            pltpu.VMEM((1, FINE), F32),
            pltpu.VMEM(fine, BF16),
            pltpu.VMEM(fine, BF16),
            pltpu.VMEM(fine, BF16),
            pltpu.VMEM(fine, BF16),
            pltpu.VMEM((2, 3 * TILE, FINE), BF16),
            pltpu.VMEM((2, TILE, FINE), BF16),
            dma((4, chunks)),
            dma((8, chunks)), dma((8, chunks)), dma((8, chunks)), dma((8, chunks)),
            dma((2,)), dma((2,)), dma((8, 2)), dma((8, 2)), dma((10, 2)), dma((10, 2)),
        ],
        compiler_params=pltpu.CompilerParams(
            collective_id=0, has_side_effects=True, vmem_limit_bytes=32 * 2**20),
        name="sum_kernel",
    )(*(pltpu.with_memory_space_constraint(x, pltpu.HBM) for x in (
        alpha, perts, widths, lat_index[None], lat_weight[None], lon_index[None], lon_weight[None],
        innovation, obs_weight)))
    gradient, increment = pl.pallas_call(
        gradient_kernel,
        out_shape=[
            jax.ShapeDtypeStruct(alpha.shape, F32),
            jax.ShapeDtypeStruct(fine, F32),
        ],
        in_specs=[vmem] * 10,
        out_specs=[hbm, hbm],
        scratch_shapes=[
            pltpu.VMEM((2, GROUP * EXT, 2 * FINE), BF16),
            pltpu.VMEM((2, 2 * FINE, GROUP * TILE), BF16),
            pltpu.VMEM(alpha.shape, F32),
            dma((2, chunks)), dma,
        ],
        compiler_params=pltpu.CompilerParams(vmem_limit_bytes=32 * 2**20),
        name="gradient_kernel",
    )(alpha_v, perts_v, ph, pw, pe, res, edge, lon, lat, inc)
    return (increment, gradient)


def solution(mesh):
    placed = (
        P("ma", None, "gy", "gx"),
        P("ma", None, "gy", "gx"),
        P(),
        P("gy"),
        P("gy"),
        P("gx"),
        P("gx"),
        P(None, "gy", "gx"),
        P(None, "gy", "gx"),
    )
    return jax.shard_map(
        body,
        mesh=mesh,
        in_specs=placed,
        out_specs=(P(None, "gy", "gx"), P("ma", None, "gy", "gx")),
        check_vma=False,
    )
```

time: 67.9 us -> 51.9 us (0.76)
  Pallas kernels: 59.8 us -> 51.2 us
  local copies, waits for them, and re-layouts: 7.18 us -> 0 us
    pallas_call x2, Pallas kernels: 59.8 us -> 51.2 us  [the longest x1 43.4 us: body(): pl.pallas_call(sum_kernel, out_shape=shapes, in_specs=[hbm] * 9, out_spec...]
    unnamed x16 -> x0, local copies, waits for them, and re-layouts: 7.18 us -> none
where the time goes in v1:
time: 51.9 us; the launch traced here: 51.8 us
  Pallas kernels  51.2 us (99%)
  between operations  0.64 us (1%)
    pallas_call x1, Pallas kernels, body(): pl.pallas_call(sum_kernel, out_shape=shapes, in_specs=[hbm] * 9, out_spec...  43.4 us
    pallas_call x1, Pallas kernels, body(): pl.pallas_call(gradient_kernel, out_shape=[jax.ShapeDtypeStruct(alpha.sha...  7.8 us

profile of v1, /device:TPU:1, one launch (start us, length us, event | category | flops | bytes accessed | tf_op | source)
XLA Modules:
  0.0 51.8 jit_solution(8148461281962534830)
XLA Ops:
  0.6 43.4 %sum_kernel.1 = (f32[2,256,256]{2,1,0:T(8,128)S(1)}, f32[2,144,128]{2,1,0:T(8,128)S(1)}, f32[2,144,128]{2,1,0:T(8,128)S(1)}, bf16[40,2,16,128]{3,2,1,0:T(8,128)(...) custom-call(bf16[40,2,128,128]{3,2,1,0:T(8,128)(2,1)} %alpha_hbm.1, ...), custom_call_target="tpu_custom_call" | custom-call | tf_op jit(solution)/shard_map/sum_kernel/pallas_call | solution.py:491
  44.0 7.8 %gradient_kernel.1 = (f32[40,2,128,128]{3,2,1,0:T(8,128)}, f32[2,256,256]{2,1,0:T(8,128)}) custom-call(bf16[40,2,128,128]{3,2,1,0:T(8,128)(2,1)S(1)} %get-tuple-element.14.alpha, bf16[40,2,128,128]{3,2,1,0:T(8,128)(2,1)S(1)} %get-tuple-element.15.perts, bf16[40,2,16,128]{3,2,1,0:T(8,128)(2,1)S(1)} %get-tuple-element.16.ph, ...), custom_call_target="tpu_custom_call" | custom-call | tf_op jit(solution)/shard_map/gradient_kernel/pallas_call | solution.py:542
